TPU v7x, 32 devices: a whole 2x2x4 slice. The times are simulated.
32 devices in a mesh: row: 4 (over y, x), col: 8 (over z, core).
Axes of the slice: x: 2, y: 2, z: 4, core: 2. Of those that a mesh axis runs over, the one named last changes fastest.
Arguments:
- mlp_param: float32 [6144, 24576], P('row', 'col'), may hold values from -250 to 250
- mlp_grad: bfloat16 [6144, 24576], P('row', 'col'), may hold values from -250 to 250
- mlp_row_state: float32 [6144], P('row'), may hold values from 0.03 to 2.7
- mlp_col_state: float32 [24576], P('col'), may hold values from 0.02 to 0.3
- attn_param: float32 [6144, 6144], P('row', 'col'), may hold values from -250 to 250
- attn_grad: bfloat16 [6144, 6144], P('row', 'col'), may hold values from -250 to 250
- attn_row_state: float32 [6144], P('row'), may hold values from 0.03 to 2.7
- attn_col_state: float32 [6144], P('col'), may hold values from 0.02 to 0.3
Outputs:
- mlp_param_new: float32 [6144, 24576], P('row', 'col')
- attn_param_new: float32 [6144, 6144], P('row', 'col')
- mlp_row_new: float32 [6144], P('row')
- mlp_col_new: float32 [24576], P('col')
- attn_row_new: float32 [6144], P('row')
- attn_col_new: float32 [6144], P('col')
- attn_copy: bfloat16 [6144, 6144], P(None, 'col')
All inputs are finite; a program needn't handle non-finite values.
Results may differ from a plain program's by a relative error of at most 0.0004.
Values may be sent and summed in bfloat16 or wider, within the bound.
A program may use at most 128 MiB of HBM per device.

v0:
```python
import jax
import jax.numpy as jnp
from jax import lax
from jax.sharding import PartitionSpec as P

STEP = 4
TINY_SQUARE = 1e-30
LEARN_RATE = 0.05
DECAY_POWER = 0.8


def local(
    mlp_param,
    mlp_grad,
    mlp_row_state,
    mlp_col_state,
    attn_param,
    attn_grad,
    attn_row_state,
    attn_col_state,
):
    keep_rate = 1.0 - STEP ** (-DECAY_POWER)
    block_rows = mlp_grad.shape[0]
    rows_total = block_rows * lax.axis_size("row")
    mlp_width = mlp_grad.shape[1] * lax.axis_size("col")
    attn_width = attn_grad.shape[1] * lax.axis_size("col")
    mlp_count = float(rows_total * mlp_width)
    attn_count = float(rows_total * attn_width)
    mlp_square = jnp.square(mlp_grad.astype(jnp.float32)) + TINY_SQUARE
    attn_square = jnp.square(attn_grad.astype(jnp.float32)) + TINY_SQUARE
    param_local = (jnp.sum(jnp.square(mlp_param)), jnp.sum(jnp.square(attn_param)))
    param_mlp, param_attn = lax.psum((param_local[0], param_local[1]), ("row", "col"))
    row_mlp, row_attn = lax.psum((jnp.sum(mlp_square, axis=1), jnp.sum(attn_square, axis=1)), "col")
    mlp_rows_new = keep_rate * mlp_row_state + (1.0 - keep_rate) * (row_mlp / mlp_width)
    attn_rows_new = keep_rate * attn_row_state + (1.0 - keep_rate) * (row_attn / attn_width)
    col_mlp, col_attn = lax.psum((jnp.sum(mlp_square, axis=0), jnp.sum(attn_square, axis=0)), "row")
    mlp_cols_new = keep_rate * mlp_col_state + (1.0 - keep_rate) * (col_mlp / rows_total)
    attn_cols_new = keep_rate * attn_col_state + (1.0 - keep_rate) * (col_attn / rows_total)
    mlp_raw = mlp_grad.astype(jnp.float32) / jnp.sqrt(mlp_rows_new[:, None] * mlp_cols_new[None, :])
    attn_raw = attn_grad.astype(jnp.float32) / jnp.sqrt(
        attn_rows_new[:, None] * attn_cols_new[None, :]
    )
    clip_local = (jnp.sum(jnp.square(mlp_raw)), jnp.sum(jnp.square(attn_raw)))
    clip_mlp, clip_attn = lax.psum((clip_local[0], clip_local[1]), ("row", "col"))
    mlp_clip = jnp.maximum(1.0, jnp.sqrt(clip_mlp / mlp_count))
    attn_clip = jnp.maximum(1.0, jnp.sqrt(clip_attn / attn_count))
    mlp_step = LEARN_RATE * jnp.sqrt(param_mlp / mlp_count)
    attn_step = LEARN_RATE * jnp.sqrt(param_attn / attn_count)
    mlp_new = mlp_param - mlp_step * (mlp_raw / mlp_clip)
    attn_new = attn_param - attn_step * (attn_raw / attn_clip)
    weight_copy = lax.all_gather(attn_new.astype(jnp.bfloat16), "row", axis=0, tiled=True)
    return (
        mlp_new,
        attn_new,
        mlp_rows_new,
        mlp_cols_new,
        attn_rows_new,
        attn_cols_new,
        weight_copy,
    )


def solution(mesh):
    return jax.shard_map(
        local,
        mesh=mesh,
        in_specs=(
            P("row", "col"),
            P("row", "col"),
            P("row"),
            P("col"),
            P("row", "col"),
            P("row", "col"),
            P("row"),
            P("col"),
        ),
        out_specs=(
            P("row", "col"),
            P("row", "col"),
            P("row"),
            P("col"),
            P("row"),
            P("col"),
            P(None, "col"),
        ),
        check_vma=False,
    )
```

profile of v0, /device:TPU:0, one launch (start us, length us, event | category | flops | bytes accessed | tf_op | source)
XLA Modules:
  0.0 249.6 jit_solution(1990881381430585324)
XLA Ops:
  7.2 0.0 all-gather.2.cloned.1.call-start
  7.2 12.0 %multiply_reduce_fusion.1 = f32[]{:T(128)} fusion(f32[1536,3072]{1,0:T(8,128)} %param.8), kind=kLoop, calls=%fused_computation.7 | loop fusion | flops 9437183 | bytes 18874372 | tf_op jit(solution)/shard_map/reduce_sum | solution.py:31
  19.2 1.0 fusion.5
  20.2 0.0 copy-start.8
  20.2 0.0 slice-start
  20.2 13.0 %fusion.2 = (f32[1536]{0:T(1024)S(1)}, f32[3072]{0:T(1024)S(1)}) fusion(bf16[1536,3072]{1,0:T(8,128)(2,1)} %param.9), kind=kLoop, calls=%fused_computation.4 | loop fusion | flops 23588352 | bytes 9455616 | tf_op jit(solution)/shard_map/reduce_sum | solution.py:33
  33.2 30.3 %all-reduce.1 = (f32[1536]{0:T(1024)S(1)}, f32[1536]{0:T(1024)S(1)}) all-reduce(f32[1536]{0:T(1024)S(1)} %get-tuple-element.7, f32[1536]{0:T(1024)S(1)} %get-tuple-element.9), channel_id=1, replica_groups=mesh['row'=4,'col'=8] {'col'}, use_global_device_ids=true, to_apply=%region_3.0 | all-reduce | flops 3072 | bytes 24576 | tf_op jit(solution)/shard_map/psum | solution.py:33
  63.5 16.0 %all-reduce.2 = (f32[3072]{0:T(1024)S(1)}, f32[768]{0:T(1024)S(1)}) all-reduce(f32[3072]{0:T(1024)S(1)} %get-tuple-element.8, f32[768]{0:T(1024)S(1)} %get-tuple-element.10), channel_id=1, replica_groups=mesh['row'=4,'col'=8] {'row'}, use_global_device_ids=true, to_apply=%region_5.0 | all-reduce | flops 3840 | bytes 30720 | tf_op jit(solution)/shard_map/psum | solution.py:36
  79.6 0.0 copy-done.5
  79.6 0.0 copy-start.1
  79.6 0.0 copy-start.2
  79.6 0.0 copy-start.3
  79.7 0.0 slice-start.1
  79.7 9.5 %multiply_reduce_fusion = f32[]{:T(128)} fusion(bf16[1536,3072]{1,0:T(8,128)(2,1)} %param.9, f32[3072]{0:T(1024)S(1)} %multiply_add_fusion, f32[1536]{0:T(1024)S(1)} %get-tuple-element.32), kind=kLoop, calls=%fused_computation.6 | loop fusion | flops 23592960 | bytes 9455620 | tf_op jit(solution)/shard_map/reduce_sum | solution.py:43
  89.2 2.5 %multiply_reduce_fusion.2 = f32[]{:T(128)} fusion(bf16[1536,768]{1,0:T(8,128)(2,1)S(1)} %copy-done, f32[768]{0:T(1024)S(1)} %multiply_add_fusion.3, f32[1536]{0:T(1024)S(1)} %get-tuple-element.34), kind=kLoop, calls=%fused_computation.14 | loop fusion | flops 5898239 | bytes 2368516 | tf_op jit(solution)/shard_map/reduce_sum | solution.py:43
  91.7 1.9 multiply_reduce_fusion.3
  93.6 37.2 %all-reduce = (f32[]{:T(128)}, f32[]{:T(128)}, f32[]{:T(128)}, f32[]{:T(128)}) all-reduce(f32[]{:T(128)} %multiply_reduce_fusion, f32[]{:T(128)} %multiply_reduce_fusion.1, f32[]{:T(128)} %multiply_reduce_fusion.2, f32[]{:T(128)} %multiply_reduce_fusion.3), channel_id=1, replica_groups=mesh['row'=4,'col'=8] {'row','col'}, use_global_device_ids=true, to_apply=%region_7.0 | all-reduce | flops 4 | bytes 32 | tf_op jit(solution)/shard_map/psum | solution.py:44
  132.3 5.4 %fusion.6 = (bf16[1536,768]{1,0:T(8,128)(2,1)}, f32[1536,768]{1,0:T(8,128)}) fusion(f32[1536,768]{1,0:T(8,128)} %param.12, f32[]{:T(128)S(6)} %max.7, f32[768]{0:T(1024)S(1)} %multiply_add_fusion.3, f32[1536]{0:T(1024)S(1)} %get-tuple-element.34, bf16[1536,768]{1,0:T(8,128)(2,1)S(1)} %copy-done, f32[]{:T(128)S(6)} %mul.97), kind=kLoop, calls=%fused_computation.20 | loop fusion | flops 8257536 | bytes 14165000 | tf_op jit(solution)/shard_map/convert_element_type | solution.py:51
  137.7 0.0 all-gather.2.cloned.1.call-update
  139.1 0.0 copy-done.1
  139.1 0.0 copy-done.3
  139.1 19.4 %multiply_subtract_fusion = f32[1536,3072]{1,0:T(8,128)} fusion(f32[1536,3072]{1,0:T(8,128)} %param.8, bf16[1536,3072]{1,0:T(8,128)(2,1)} %param.9, f32[]{:T(128)S(6)} %max.6, f32[3072]{0:T(1024)S(1)} %multiply_add_fusion, f32[1536]{0:T(1024)S(1)} %get-tuple-element.32, f32[]{:T(128)S(6)} %mul.84), kind=kLoop, calls=%fused_computation.5 | loop fusion | flops 28311552 | bytes 47204360 | tf_op jit(solution)/shard_map/sub | solution.py:49
  158.5 76.3 %all-gather.2.cloned.1.call-done = bf16[6144,768]{1,0:T(8,128)(2,1)} async-done(((bf16[1536,768]{1,0:T(8,128)(2,1)}), bf16[6144,768]{1,0:T(8,128)(2,1)}) %all-gather.2.cloned.1.call-update) | async-done | bytes 9437200 | tf_op jit(solution)/shard_map/all_gather | solution.py:51
  234.8 8.0 %copy.16 = bf16[6144,768]{1,0:T(8,128)(2,1)} copy(bf16[6144,768]{1,0:T(8,128)(2,1)} %all-gather.2.cloned.1.call-done) | data formatting | bytes 18874368
  (17 shorter events, 0.0 us)
Async XLA Ops:
  7.2 12.0 %copy-start = (bf16[1536,768]{1,0:T(8,128)(2,1)S(1)}, bf16[1536,768]{1,0:T(8,128)(2,1)}, u32[]{:S(2)}) copy-start(bf16[1536,768]{1,0:T(8,128)(2,1)} %param.13) | copy-start | bytes 7077892
  7.2 227.6 %all-gather.2.cloned.1.call-start = ((), (), s32[]{:S(2)}) async-start(), calls=%async_computation | async-start | bytes 11796480 | tf_op jit(solution)/shard_map/all_gather | solution.py:51
  19.2 60.4 %copy-start.5 = (f32[3072]{0:T(1024)S(1)}, f32[3072]{0:T(1024)}, u32[]{:S(2)}) copy-start(f32[3072]{0:T(1024)} %param.11) | copy-start | bytes 36868
  19.2 60.4 %copy-start.6 = (f32[1536]{0:T(1024)S(1)}, f32[1536]{0:T(1024)}, u32[]{:S(2)}) copy-start(f32[1536]{0:T(1024)} %param.14) | copy-start | bytes 18436
  19.2 60.4 %copy-start.7 = (f32[1536]{0:T(1024)S(1)}, f32[1536]{0:T(1024)}, u32[]{:S(2)}) copy-start(f32[1536]{0:T(1024)} %param.10) | copy-start | bytes 18436
  20.2 69.0 %copy-start.8 = (f32[768]{0:T(1024)S(1)}, f32[768]{0:T(1024)}, u32[]{:S(2)}) copy-start(f32[768]{0:T(1024)} %param.15) | copy-start | bytes 9220
  20.2 71.5 %slice-start = ((s8[4718592]{0:T(1024)(128)(4,1)}), s8[524288]{0:T(1024)(128)(4,1)S(1)}, s32[]{:S(2)}) async-start(s8[4718592]{0:T(1024)(128)(4,1)} %bitcast), calls=%async_computation.1 | async-start | bytes 1048576
  79.6 59.5 %copy-start.1 = (f32[3072]{0:T(1024)}, f32[3072]{0:T(1024)S(1)}, u32[]{:S(2)}) copy-start(f32[3072]{0:T(1024)S(1)} %multiply_add_fusion) | copy-start | bytes 36868
  79.6 58.1 %copy-start.2 = (f32[1536]{0:T(1024)}, f32[1536]{0:T(1024)S(1)}, u32[]{:S(2)}) copy-start(f32[1536]{0:T(1024)S(1)} %get-tuple-element.34) | copy-start | bytes 18436
  79.6 59.5 %copy-start.3 = (f32[1536]{0:T(1024)}, f32[1536]{0:T(1024)S(1)}, u32[]{:S(2)}) copy-start(f32[1536]{0:T(1024)S(1)} %get-tuple-element.32) | copy-start | bytes 18436
  79.7 12.1 %slice-start.1 = ((s8[4718592]{0:T(1024)(128)(4,1)}), s8[4194304]{0:T(1024)(128)(4,1)S(1)}, s32[]{:S(2)}) async-start(s8[4718592]{0:T(1024)(128)(4,1)} %bitcast), calls=%async_computation.2 | async-start | bytes 8388608
  89.2 48.5 %copy-start.4 = (f32[768]{0:T(1024)}, f32[768]{0:T(1024)S(1)}, u32[]{:S(2)}) copy-start(f32[768]{0:T(1024)S(1)} %multiply_add_fusion.3) | copy-start | bytes 9220
Sparse Core Ops, SparseCore 0:
  137.8 96.8 all-gather.1
where the time goes:
time: 250 us
  blocking collectives  83.6 us (33%)
  waiting for transfers between devices  76.3 us (31%)
  other arithmetic  64.7 us (26%)
  between operations  17 us (7%)
  local copies, waits for them, and re-layouts  8.09 us (3%)
    all_gather x1, waiting for transfers between devices, local(): lax.all_gather(attn_new.astype(jnp.bfloat16), 'row', axis=0, tiled=True)  76.3 us
    psum x1, blocking collectives, local(): lax.psum((clip_local[0], clip_local[1]), ('row', 'col'))  37.2 us
    psum x1, blocking collectives, local(): lax.psum((jnp.sum(mlp_square, axis=1), jnp.sum(attn_square, axis=1)), 'col')  30.3 us
    sub x1, other arithmetic, local(): mlp_new = mlp_param - mlp_step * (mlp_raw / mlp_clip)  19.4 us
    psum x1, blocking collectives, local(): lax.psum((jnp.sum(mlp_square, axis=0), jnp.sum(attn_square, axis=0)), 'row')  16 us
    reduce_sum x1, other arithmetic, local(): jnp.sum(mlp_square, axis=1)  13 us
    reduce_sum x2, other arithmetic, local(): clip_local = (jnp.sum(jnp.square(mlp_raw)), jnp.sum(jnp.square(attn_raw)))  12.1 us
    reduce_sum x1, other arithmetic, local(): jnp.sum(jnp.square(mlp_param))  12 us
  transfers between devices with their start and end apart: 1, of which 1 were waited for; matrix products, arithmetic and copies ran while one was open for 8% of the time, Pallas kernels for 0%

commit v1 on v0

--- a/solution.py
+++ b/solution.py
@@ -41,7 +41,7 @@
         attn_rows_new[:, None] * attn_cols_new[None, :]
     )
     clip_local = (jnp.sum(jnp.square(mlp_raw)), jnp.sum(jnp.square(attn_raw)))
-    clip_mlp, clip_attn = lax.psum((clip_local[0], clip_local[1]), ("row", "col"))
+    clip_mlp, clip_attn = lax.psum(lax.psum((clip_local[0], clip_local[1]), "col"), "row")
     mlp_clip = jnp.maximum(1.0, jnp.sqrt(clip_mlp / mlp_count))
     attn_clip = jnp.maximum(1.0, jnp.sqrt(clip_attn / attn_count))
     mlp_step = LEARN_RATE * jnp.sqrt(param_mlp / mlp_count)

time: 250 us -> 273 us (1.092)
  blocking collectives: 83.6 us -> 107 us
  waiting for transfers between devices: 76.3 us -> 73.2 us
    psum x1 -> x3, blocking collectives: 37.2 us -> 64.8 us  [the longest x1 42.5 us: local(): lax.psum((param_local[0], param_local[1]), ('row', 'col'))]
    psum x1, blocking collectives: 30.3 us -> 26.8 us  [local(): lax.psum((jnp.sum(mlp_square, axis=1), jnp.sum(attn_square, axis=1)), 'col')]
    all_gather x1, waiting for transfers between devices: 76.3 us -> 73.1 us  [local(): lax.all_gather(attn_new.astype(jnp.bfloat16), 'row', axis=0, tiled=True)]
    unnamed x23 -> x19, local copies, waits for them, and re-layouts: 8.09 us -> 8.07 us
  transfers between devices with their start and end apart: 1 -> 1, of which waited for: 1 -> 1; matrix products, arithmetic and copies ran while one was open for 8% -> 7% of each run, Pallas kernels for 0% -> 0%
where the time goes in v1:
time: 273 us
  blocking collectives  107 us (39%)
  waiting for transfers between devices  73.2 us (27%)
  other arithmetic  67 us (25%)
  between operations  16.9 us (6%)
  local copies, waits for them, and re-layouts  8.07 us (3%)
    all_gather x1, waiting for transfers between devices, local(): lax.all_gather(attn_new.astype(jnp.bfloat16), 'row', axis=0, tiled=True)  73.1 us
    psum x1, blocking collectives, local(): lax.psum((param_local[0], param_local[1]), ('row', 'col'))  42.5 us
    psum x1, blocking collectives, local(): lax.psum((jnp.sum(mlp_square, axis=1), jnp.sum(attn_square, axis=1)), 'col')  26.8 us
    sub x1, other arithmetic, local(): mlp_new = mlp_param - mlp_step * (mlp_raw / mlp_clip)  19.6 us
    psum x1, blocking collectives, local(): lax.psum((jnp.sum(mlp_square, axis=0), jnp.sum(attn_square, axis=0)), 'row')  15.9 us
    psum x1, blocking collectives, local(): lax.psum((clip_local[0], clip_local[1]), 'col')  14.2 us
    reduce_sum x1, other arithmetic, local(): jnp.sum(mlp_square, axis=1)  13.1 us
    reduce_sum x2, other arithmetic, local(): clip_local = (jnp.sum(jnp.square(mlp_raw)), jnp.sum(jnp.square(attn_raw)))  11.9 us
  transfers between devices with their start and end apart: 1, of which 1 were waited for; matrix products, arithmetic and copies ran while one was open for 7% of the time, Pallas kernels for 0%

profile of v1, /device:TPU:0, one launch (start us, length us, event | category | flops | bytes accessed | tf_op | source)
XLA Modules:
  0.0 272.6 jit_solution(15233676696966110958)
XLA Ops:
  7.2 0.0 all-gather.2.cloned.1.call-start
  7.2 4.2 %multiply_reduce_fusion.3 = f32[]{:T(128)} fusion(f32[1536,768]{1,0:T(8,128)} %param.12), kind=kLoop, calls=%fused_computation.15 | loop fusion | flops 2359295 | bytes 4718596 | tf_op jit(solution)/shard_map/reduce_sum | solution.py:31
  11.4 11.8 %multiply_reduce_fusion.1 = f32[]{:T(128)} fusion(f32[1536,3072]{1,0:T(8,128)} %param.8), kind=kLoop, calls=%fused_computation.7 | loop fusion | flops 9437183 | bytes 18874372 | tf_op jit(solution)/shard_map/reduce_sum | solution.py:31
  23.2 13.1 %fusion.2 = (f32[1536]{0:T(1024)S(1)}, f32[3072]{0:T(1024)S(1)}) fusion(bf16[1536,3072]{1,0:T(8,128)(2,1)} %param.9), kind=kLoop, calls=%fused_computation.4 | loop fusion | flops 23588352 | bytes 9455616 | tf_op jit(solution)/shard_map/reduce_sum | solution.py:33
  36.3 0.0 copy-done
  36.3 1.0 fusion.5
  37.3 42.5 %all-reduce = (f32[]{:T(128)}, f32[]{:T(128)}) all-reduce(f32[]{:T(128)} %multiply_reduce_fusion.1, f32[]{:T(128)} %multiply_reduce_fusion.3), channel_id=1, replica_groups=mesh['row'=4,'col'=8] {'row','col'}, use_global_device_ids=true, to_apply=%region_1.0 | all-reduce | flops 2 | bytes 16 | tf_op jit(solution)/shard_map/psum | solution.py:32
  80.4 26.8 %all-reduce.2 = (f32[1536]{0:T(1024)S(1)}, f32[1536]{0:T(1024)S(1)}) all-reduce(f32[1536]{0:T(1024)S(1)} %get-tuple-element.7, f32[1536]{0:T(1024)S(1)} %get-tuple-element.9), channel_id=1, replica_groups=mesh['row'=4,'col'=8] {'col'}, use_global_device_ids=true, to_apply=%region_3.0 | all-reduce | flops 3072 | bytes 24576 | tf_op jit(solution)/shard_map/psum | solution.py:33
  107.3 15.9 %all-reduce.4 = (f32[3072]{0:T(1024)S(1)}, f32[768]{0:T(1024)S(1)}) all-reduce(f32[3072]{0:T(1024)S(1)} %get-tuple-element.8, f32[768]{0:T(1024)S(1)} %get-tuple-element.10), channel_id=1, replica_groups=mesh['row'=4,'col'=8] {'row'}, use_global_device_ids=true, to_apply=%region_5.0 | all-reduce | flops 3840 | bytes 30720 | tf_op jit(solution)/shard_map/psum | solution.py:36
  123.1 0.0 copy-done.5
  123.1 0.0 copy-start.1
  123.2 0.0 copy-done.6
  123.2 0.0 copy-start.2
  123.2 0.0 copy-start.3
  123.2 9.4 %multiply_reduce_fusion = f32[]{:T(128)} fusion(bf16[1536,3072]{1,0:T(8,128)(2,1)} %param.9, f32[3072]{0:T(1024)S(1)} %multiply_add_fusion, f32[1536]{0:T(1024)S(1)} %get-tuple-element.34), kind=kLoop, calls=%fused_computation.6 | loop fusion | flops 23592960 | bytes 9455620 | tf_op jit(solution)/shard_map/reduce_sum | solution.py:43
  132.6 2.5 multiply_reduce_fusion.2
  135.2 14.2 %all-reduce.1 = (f32[]{:T(128)}, f32[]{:T(128)}) all-reduce(f32[]{:T(128)} %multiply_reduce_fusion, f32[]{:T(128)} %multiply_reduce_fusion.2), channel_id=1, replica_groups=mesh['row'=4,'col'=8] {'col'}, use_global_device_ids=true, to_apply=%region_7.0 | all-reduce | flops 2 | bytes 16 | tf_op jit(solution)/shard_map/psum | solution.py:44
  149.4 8.1 %all-reduce.3 = (f32[]{:T(128)}, f32[]{:T(128)}) all-reduce(f32[]{:T(128)} %get-tuple-element.13, f32[]{:T(128)} %get-tuple-element.14), channel_id=1, replica_groups=mesh['row'=4,'col'=8] {'row'}, use_global_device_ids=true, to_apply=%region_8.0 | all-reduce | flops 2 | bytes 16 | tf_op jit(solution)/shard_map/psum | solution.py:44
  158.2 5.4 %fusion.6 = (bf16[1536,768]{1,0:T(8,128)(2,1)}, f32[1536,768]{1,0:T(8,128)}) fusion(f32[1536,768]{1,0:T(8,128)} %param.12, f32[]{:T(128)S(6)} %max.7, f32[768]{0:T(1024)S(1)} %multiply_add_fusion.3, f32[1536]{0:T(1024)S(1)} %get-tuple-element.36, bf16[1536,768]{1,0:T(8,128)(2,1)S(1)} %copy-done, f32[]{:T(128)S(6)} %mul.97), kind=kLoop, calls=%fused_computation.20 | loop fusion | flops 8257536 | bytes 14165000 | tf_op jit(solution)/shard_map/convert_element_type | solution.py:51
  163.6 0.0 all-gather.2.cloned.1.call-update
  163.6 0.0 copy-done.4
  165.0 19.6 %multiply_subtract_fusion = f32[1536,3072]{1,0:T(8,128)} fusion(f32[1536,3072]{1,0:T(8,128)} %param.8, bf16[1536,3072]{1,0:T(8,128)(2,1)} %param.9, f32[]{:T(128)S(6)} %max.6, f32[3072]{0:T(1024)S(1)} %multiply_add_fusion, f32[1536]{0:T(1024)S(1)} %get-tuple-element.34, f32[]{:T(128)S(6)} %mul.84), kind=kLoop, calls=%fused_computation.5 | loop fusion | flops 28311552 | bytes 47204360 | tf_op jit(solution)/shard_map/sub | solution.py:49
  184.6 73.1 %all-gather.2.cloned.1.call-done = bf16[6144,768]{1,0:T(8,128)(2,1)} async-done(((bf16[1536,768]{1,0:T(8,128)(2,1)}), bf16[6144,768]{1,0:T(8,128)(2,1)}) %all-gather.2.cloned.1.call-update) | async-done | bytes 9437200 | tf_op jit(solution)/shard_map/all_gather | solution.py:51
  257.8 8.0 %copy.16 = bf16[6144,768]{1,0:T(8,128)(2,1)} copy(bf16[6144,768]{1,0:T(8,128)(2,1)} %all-gather.2.cloned.1.call-done) | data formatting | bytes 18874368
  (14 shorter events, 0.0 us)
Async XLA Ops:
  7.2 250.6 %all-gather.2.cloned.1.call-start = ((), (), s32[]{:S(2)}) async-start(), calls=%async_computation | async-start | bytes 11796480 | tf_op jit(solution)/shard_map/all_gather | solution.py:51
  23.2 13.1 %copy-start = (bf16[1536,768]{1,0:T(8,128)(2,1)S(1)}, bf16[1536,768]{1,0:T(8,128)(2,1)}, u32[]{:S(2)}) copy-start(bf16[1536,768]{1,0:T(8,128)(2,1)} %param.13) | copy-start | bytes 7077892
  23.2 99.9 %copy-start.5 = (f32[3072]{0:T(1024)S(1)}, f32[3072]{0:T(1024)}, u32[]{:S(2)}) copy-start(f32[3072]{0:T(1024)} %param.11) | copy-start | bytes 36868
  23.2 100.0 %copy-start.6 = (f32[1536]{0:T(1024)S(1)}, f32[1536]{0:T(1024)}, u32[]{:S(2)}) copy-start(f32[1536]{0:T(1024)} %param.14) | copy-start | bytes 18436
  23.2 100.0 %copy-start.7 = (f32[1536]{0:T(1024)S(1)}, f32[1536]{0:T(1024)}, u32[]{:S(2)}) copy-start(f32[1536]{0:T(1024)} %param.10) | copy-start | bytes 18436
  23.2 109.4 %copy-start.8 = (f32[768]{0:T(1024)S(1)}, f32[768]{0:T(1024)}, u32[]{:S(2)}) copy-start(f32[768]{0:T(1024)} %param.15) | copy-start | bytes 9220
  123.1 41.8 %copy-start.1 = (f32[3072]{0:T(1024)}, f32[3072]{0:T(1024)S(1)}, u32[]{:S(2)}) copy-start(f32[3072]{0:T(1024)S(1)} %multiply_add_fusion) | copy-start | bytes 36868
  123.2 40.4 %copy-start.2 = (f32[1536]{0:T(1024)}, f32[1536]{0:T(1024)S(1)}, u32[]{:S(2)}) copy-start(f32[1536]{0:T(1024)S(1)} %get-tuple-element.36) | copy-start | bytes 18436
  123.2 41.8 %copy-start.3 = (f32[1536]{0:T(1024)}, f32[1536]{0:T(1024)S(1)}, u32[]{:S(2)}) copy-start(f32[1536]{0:T(1024)S(1)} %get-tuple-element.34) | copy-start | bytes 18436
  132.6 31.0 %copy-start.4 = (f32[768]{0:T(1024)}, f32[768]{0:T(1024)S(1)}, u32[]{:S(2)}) copy-start(f32[768]{0:T(1024)S(1)} %multiply_add_fusion.3) | copy-start | bytes 9220
Sparse Core Ops, SparseCore 0:
  163.7 93.9 all-gather.1
